TPU v7x, 32 devices: a whole 2x2x4 slice. The times are simulated.
32 devices in a mesh: row: 8 (over y, x, core), col: 4 (over z).
Axes of the slice: x: 2, y: 2, z: 4, core: 2. Of those that a mesh axis runs over, the one named last changes fastest.
Arguments:
- queries: bfloat16 [256, 32, 128], P(('row', 'col')), may hold values from -1 to 1
- documents: bfloat16 [256, 128, 128], P(('row', 'col')), may hold values from -1 to 1
- lengths: int32 [256], P(('row', 'col')), may hold values from 1 to 128
- positives: int32 [256], P(('row', 'col')), may hold values from 0 to 255
Outputs:
- query_loss: float32 [256], P(('row', 'col'))
All inputs are finite; a program needn't handle non-finite values.
Results may differ from a plain program's by a relative error of at most 0.0003.
Values may be sent and summed in bfloat16 or wider, within the bound.
A program may use at most 64 MiB of HBM per device.

v0:
```python
import jax
import jax.numpy as jnp
from jax import lax
from jax.sharding import PartitionSpec as P

neg_fill = -1e30


def maxsim(query_rows, doc_rows, doc_lengths, group_docs):
    query_count = query_rows.shape[0]
    query_tokens = query_rows.shape[1]
    query_flat = query_rows.reshape(query_count * query_tokens, query_rows.shape[2])
    doc_count = doc_rows.shape[0]
    slot_count = doc_rows.shape[1]
    group_count = doc_count // group_docs
    grouped_docs = doc_rows.reshape(group_count, group_docs * slot_count, doc_rows.shape[2])
    grouped_lengths = doc_lengths.astype(jnp.float32).reshape(group_count, group_docs)
    token_slots = jnp.arange(slot_count, dtype=jnp.float32)

    def one_group(group_pair):
        block_docs, block_lengths = group_pair
        similar = lax.dot_general(
            query_flat, block_docs, (((1,), (1,)), ((), ())), preferred_element_type=jnp.float32
        )
        similar = similar.reshape(query_count * query_tokens, group_docs, slot_count)
        valid = token_slots[None, :] < block_lengths[:, None]
        similar = jnp.where(valid[None, :, :], similar, neg_fill)
        best = jnp.max(similar, axis=2).reshape(query_count, query_tokens, group_docs)
        return jnp.sum(best, axis=1)

    block_scores = lax.map(one_group, (grouped_docs, grouped_lengths))
    return jnp.transpose(block_scores, (1, 0, 2)).reshape(query_count, doc_count)


def finish(owner_scores, doc_ids, positives):
    peak_score = jnp.max(owner_scores, axis=1, keepdims=True)
    log_total = peak_score[:, 0] + jnp.log(jnp.sum(jnp.exp(owner_scores - peak_score), axis=1))
    positive_score = jnp.sum(
        jnp.where(doc_ids[None, :] == positives[:, None], owner_scores, 0.0), axis=1
    )
    return log_total - positive_score


def local(queries, documents, lengths, positives):
    per_device = queries.shape[0]
    row_count = lax.axis_size("row")
    col_count = lax.axis_size("col")
    length_wire = lengths.astype(jnp.bfloat16)
    doc_group, length_group = (
        lax.all_gather(documents, "col", axis=0, tiled=True),
        lax.all_gather(length_wire, "col", axis=0, tiled=True),
    )
    block_scores = maxsim(
        lax.all_gather(queries, "row", axis=0, tiled=True), doc_group, length_group, per_device
    )
    owner_scores = lax.all_to_all(block_scores, "row", split_axis=0, concat_axis=1, tiled=True)
    doc_ids = jnp.arange(row_count * col_count * per_device, dtype=jnp.int32)
    query_loss = finish(owner_scores, doc_ids, positives)
    return query_loss


def solution(mesh):
    placed = (
        P(("row", "col"), None, None),
        P(("row", "col"), None, None),
        P(("row", "col")),
        P(("row", "col")),
    )
    return jax.shard_map(
        local, mesh=mesh, in_specs=placed, out_specs=P(("row", "col")), check_vma=False
    )
```

profile of v0, /device:TPU:0, one launch (start us, length us, event | category | flops | bytes accessed | tf_op | source)
XLA Modules:
  0.0 68.4 jit_solution(5218086903122831888)
XLA Ops:
  6.5 0.7 %all-gather.2.cloned.1.call-update = ((bf16[8,128,128]{2,1,0:T(8,128)(2,1)}), bf16[32,128,128]{2,1,0:T(8,128)(2,1)}) async-update(((), (), s32[]{:S(2)}) %all-gather.2.cloned.1.call-start, bf16[8,128,128]{2,1,0:T(8,128)(2,1)} %param.7) | async-update | bytes 1572888
  7.3 0.7 convert_element_type.4
  7.9 1.2 %dynamic-slice = u32[1]{0:T(128)} dynamic-slice(u32[32]{0:T(128)} %constant.32, u32[]{:T(128)S(6)} %add.11), dynamic_slice_sizes={1} | dynamic-slice | bytes 12
  9.8 0.2 dynamic-update-slice
  10.1 13.7 %all-reduce = bf16[32]{0:T(256)(128)(2,1)S(1)} all-reduce(bf16[32]{0:T(256)(128)(2,1)S(1)} %dynamic-update-slice), channel_id=1, replica_groups=mesh['row'=8,'col'=4] {'col'}, use_global_device_ids=true, to_apply=%add | all-reduce | flops 32 | bytes 128
  23.7 0.1 reshape.79
  23.8 10.1 %all_gather.11 = bf16[64,32,128]{2,1,0:T(8,128)(2,1)S(1)} all-gather(bf16[8,32,128]{2,1,0:T(8,128)(2,1)} %param.6), channel_id=1, replica_groups=mesh['row'=8,'col'=4] {'row'}, dimensions={0}, use_global_device_ids=true | all-gather | bytes 589824 | tf_op jit(solution)/shard_map/all_gather | solution.py:54
  34.0 5.8 %all-gather.2.cloned.1.call-done = bf16[32,128,128]{2,1,0:T(8,128)(2,1)} async-done(((bf16[8,128,128]{2,1,0:T(8,128)(2,1)}), bf16[32,128,128]{2,1,0:T(8,128)(2,1)}) %all-gather.2.cloned.1.call-update) | async-done | bytes 1048592 | tf_op jit(solution)/shard_map/all_gather | solution.py:50
  39.7 10.4 %while.11 = (s32[]{:T(128)}, f32[4,64,8]{1,2,0:T(8,128)S(1)}, f32[4,8]{1,0:T(4,128)S(1)}, bf16[4,1024,128]{2,1,0:T(8,128)(2,1)}, bf16[2048,128]{1,0:T(8,128)(2,1)S(1)}, /*index=5*/s32[]{:T(128)}, f32[]{:T(128)}) while((s32[]{:T(128)}, f32[4,64,8]{1,2,0:T(8,128)S(1)}, f32[4,8]{1,0:T(4,128)S(1)}, bf16[4,1024,128]{2,1,0:T(8,128)(2,1)}, ...), condition=%wide.region_3.4_spmd.clone, body=%wide.region_0.3_spmd.clone.sunk | while | flops 541065728 | bytes 1061561 | solution.py:31
  39.7 0.1 iota_compare_fusion.2
  39.8 2.2 %select_reduce_fusion.2 = f32[2048,8]{0,1:T(8,128)S(1)} fusion(pred[8,128]{1,0:T(8,128)(4,1)S(1)} %iota_compare_fusion.2, bf16[2048,128]{1,0:T(8,128)(2,1)S(1)} %get-tuple-element.111, bf16[4,1024,128]{2,1,0:T(8,128)(2,1)} %get-tuple-element.110, s32[]{:T(128)} %get-tuple-element.100), kind=kOutput, calls=%fused_computation.1.clone.1 | convolution fusion | flops 541048832 | bytes 853504 | tf_op jit(solution)/shard_map/while/body/eval_jaxpr/dot_general | solution.py:22
  42.0 0.1 reshape.90
  42.2 0.1 reduce_sum.33
  42.4 2.2 %select_reduce_fusion.2 = f32[2048,8]{0,1:T(8,128)S(1)} fusion(pred[8,128]{1,0:T(8,128)(4,1)S(1)} %iota_compare_fusion.2, bf16[2048,128]{1,0:T(8,128)(2,1)S(1)} %get-tuple-element.111, bf16[4,1024,128]{2,1,0:T(8,128)(2,1)} %get-tuple-element.110, s32[]{:T(128)} %get-tuple-element.100), kind=kOutput, calls=%fused_computation.1.clone.1 | convolution fusion | flops 541048832 | bytes 853504 | tf_op jit(solution)/shard_map/while/body/eval_jaxpr/dot_general | solution.py:22
  44.7 0.1 reshape.90
  44.8 0.1 reduce_sum.33
  45.0 2.2 %select_reduce_fusion.2 = f32[2048,8]{0,1:T(8,128)S(1)} fusion(pred[8,128]{1,0:T(8,128)(4,1)S(1)} %iota_compare_fusion.2, bf16[2048,128]{1,0:T(8,128)(2,1)S(1)} %get-tuple-element.111, bf16[4,1024,128]{2,1,0:T(8,128)(2,1)} %get-tuple-element.110, s32[]{:T(128)} %get-tuple-element.100), kind=kOutput, calls=%fused_computation.1.clone.1 | convolution fusion | flops 541048832 | bytes 853504 | tf_op jit(solution)/shard_map/while/body/eval_jaxpr/dot_general | solution.py:22
  47.3 0.1 reshape.90
  47.4 0.1 reduce_sum.33
  47.7 2.2 %select_reduce_fusion.2 = f32[2048,8]{0,1:T(8,128)S(1)} fusion(pred[8,128]{1,0:T(8,128)(4,1)S(1)} %iota_compare_fusion.2, bf16[2048,128]{1,0:T(8,128)(2,1)S(1)} %get-tuple-element.111, bf16[4,1024,128]{2,1,0:T(8,128)(2,1)} %get-tuple-element.110, s32[]{:T(128)} %get-tuple-element.100), kind=kOutput, calls=%fused_computation.1.clone.1 | convolution fusion | flops 541048832 | bytes 853504 | tf_op jit(solution)/shard_map/while/body/eval_jaxpr/dot_general | solution.py:22
  49.9 0.1 reshape.90
  50.0 0.1 reduce_sum.33
  50.2 0.1 all_to_all.12
  50.3 0.1 copy.6
  50.4 0.7 %reshape.87 = f32[8,1,256]{2,1,0:T(1,128)} reshape(f32[8,8,32]{2,1,0:T(8,128)S(1)} %copy.6) | data formatting | bytes 16384
  51.1 3.6 %all-to-all-start = ((f32[8,1,256]{2,1,0:T(1,128)}), f32[8,1,256]{2,1,0:T(1,128)S(1)}, u32[]{:S(2)}, u32[]{:S(2)}) async-start(f32[8,1,256]{2,1,0:T(1,128)} %reshape.87), calls=%async_computation | async-start | bytes 16384 | tf_op jit(solution)/shard_map/all_to_all | solution.py:56
  54.7 4.7 %all-to-all-done = f32[8,1,256]{2,1,0:T(1,128)S(1)} async-done(((f32[8,1,256]{2,1,0:T(1,128)}), f32[8,1,256]{2,1,0:T(1,128)S(1)}, u32[]{:S(2)}, u32[]{:S(2)}) %all-to-all-start) | async-done | bytes 8224 | tf_op jit(solution)/shard_map/all_to_all | solution.py:56
  59.4 0.5 broadcast.37
  59.9 0.7 reduce.4
  60.7 0.1 reduce_max.18
  60.8 0.2 fusion.8
  61.0 0.5 add_subtract_fusion
  (18 shorter events, 0.4 us)
Async XLA Ops:
  6.5 33.2 %all-gather.2.cloned.1.call-start = ((), (), s32[]{:S(2)}) async-start(), calls=%async_computation.1 | async-start | bytes 1310720 | tf_op jit(solution)/shard_map/all_gather | solution.py:50
  39.7 21.1 %copy-start = (s32[8]{0:T(128)S(1)}, s32[8]{0:T(128)}, u32[]{:S(2)}) copy-start(s32[8]{0:T(128)} %param.9) | copy-start | bytes 100
  51.1 8.4 %all-to-all-start = ((f32[8,1,256]{2,1,0:T(1,128)}), f32[8,1,256]{2,1,0:T(1,128)S(1)}, u32[]{:S(2)}, u32[]{:S(2)}) async-start(f32[8,1,256]{2,1,0:T(1,128)} %reshape.87), calls=%async_computation | async-start | bytes 16384 | tf_op jit(solution)/shard_map/all_to_all | solution.py:56
Sparse Core Ops, SparseCore 0:
  8.9 30.7 all-gather.1
where the time goes:
time: 68.8 us; the launch traced here: 68.4 us
  blocking collectives  23.8 us (35%)
  between operations  14.1 us (20%)
  waiting for transfers between devices  11.2 us (16%)
  matrix products  8.9 us (13%)
  starting transfers between devices  3.65 us (5%)
  local copies, waits for them, and re-layouts  3.55 us (5%)
  other arithmetic  3.1 us (5%)
    unnamed x1, blocking collectives  13.7 us
    all_gather x1, blocking collectives, local(): lax.all_gather(queries, 'row', axis=0, tiled=True)  10.1 us
    dot_general x4, matrix products, one_group(): lax.dot_general(query_flat, block_docs, (((1,), (1,)), ((), ())), preferr...  8.9 us
    all_gather x1, waiting for transfers between devices, local(): lax.all_gather(documents, 'col', axis=0, tiled=True)  5.76 us
    all_to_all x1, waiting for transfers between devices, local(): lax.all_to_all(block_scores, 'row', split_axis=0, concat_axis=1, tiled=True)  4.7 us
    all_to_all x1, starting transfers between devices, local(): lax.all_to_all(block_scores, 'row', split_axis=0, concat_axis=1, tiled=True)  3.64 us
    unnamed x7, local copies, waits for them, and re-layouts  2.25 us
  transfers between devices with their start and end apart: 2, of which 2 were waited for; matrix products, arithmetic and copies ran while one was open for 3% of the time, Pallas kernels for 0%

commit v1 on v0

v1 whole, which is shorter than its diff:
```python
import functools

import jax
import jax.numpy as jnp
from jax import lax
from jax.experimental import pallas as pl
from jax.experimental.pallas import tpu as pltpu
from jax.sharding import PartitionSpec as P

MESH = pl.DeviceIdType.MESH
QUAD = 4
PARTS = 4


def kernel(
    Y, C, per, QT, DT,
    len_ref, pos_ref, q_ref, d_ref, out_ref,
    dbuf, qbuf, best, ones, sc_out, sc_in,
    d_send, d_recv, x_send, x_recv, r_send, r_recv, q_send, q_recv, s_send, s_recv,
):
    row, z = lax.axis_index("row"), lax.axis_index("col")
    y, k = row // QUAD, row % QUAD
    core, side = k % 2, k // 2
    core_peer = (row + 1 - 2 * core, z)
    chip_peer = (row + 2 - 4 * side, z)
    G = Y * C
    rows = per * DT
    toks = per * QT
    part = rows // PARTS

    def place(dy, dz):
        return (((y + dy) % Y) * QUAD + k, (z + dz) % C)

    def slot(dy, dz):
        return (dy % Y) * C + dz % C

    barrier = pltpu.get_barrier_semaphore()
    peers = [core_peer, chip_peer]
    peers += [place(0, d) for d in range(1, C)] + [place(e, 0) for e in range(1, Y)]
    for peer in peers:
        pl.semaphore_signal(barrier, inc=1, device_id=peer, device_id_type=MESH)

    slots = lax.broadcasted_iota(jnp.int32, (DT, d_ref.shape[1]), 0)
    for i in range(per):
        block = d_ref[i * DT:(i + 1) * DT, :].astype(jnp.float32)
        block = jnp.where(slots < len_ref[i], block, block[0:1, :])
        dbuf[0, i * DT:(i + 1) * DT, :] = block.astype(jnp.bfloat16)
    qbuf[0] = q_ref[...]
    lane = lax.broadcasted_iota(jnp.int32, ones.shape, 1)
    tok = lax.broadcasted_iota(jnp.int32, ones.shape, 0)
    ones[...] = jnp.where(lane % (QUAD * per) == tok // QT, 1.0, 0.0).astype(jnp.bfloat16)

    pl.semaphore_wait(barrier, len(peers))

    def copy(src, dst, send, recv, peer):
        return pltpu.make_async_remote_copy(
            src_ref=src, dst_ref=dst, send_sem=send, recv_sem=recv,
            device_id=peer, device_id_type=MESH,
        )

    def piece(b, i):
        return dbuf.at[b, pl.ds(i * part, part), :]

    started = []

    def go(c):
        c.start()
        started.append(c)
        return c

    got_q = {}
    for d in range(1, C):
        s = slot(0, -d)
        got_q[s] = go(copy(q_ref, qbuf.at[s], q_send.at[s], q_recv.at[s], place(0, d)))
    for e in range(1, Y):
        s = slot(-e, 0)
        got_q[s] = go(copy(q_ref, qbuf.at[s], q_send.at[s], q_recv.at[s], place(e, 0)))
    got_x = [
        go(copy(piece(0, i), piece(2, i), x_send.at[i], x_recv.at[i], chip_peer))
        for i in range(PARTS)
    ]
    got_d = go(copy(dbuf.at[0], dbuf.at[1], d_send, d_recv, core_peer))
    got_r = []

    def unit(s, b):
        sim = lax.dot_general(
            dbuf[b], qbuf[s], (((1,), (1,)), ((), ())), preferred_element_type=jnp.float32
        )
        top = jnp.max(sim.reshape(per, DT, toks), axis=1)
        best[s * per:(s + 1) * per, b * toks:(b + 1) * toks] = top

    unit(0, 0)
    got_d.wait_recv()
    unit(0, 1)
    near = [0]
    for i in range(max(PARTS, C - 1)):
        if i < PARTS:
            got_x[i].wait_recv()
            got_r.append(go(copy(piece(2, i), piece(3, i), r_send.at[i], r_recv.at[i], core_peer)))
        if i < C - 1:
            s = slot(0, -(i + 1))
            got_q[s].wait_recv()
            for e in range(1, Y):
                t = slot(-e, -(i + 1))
                got_q[t] = go(copy(qbuf.at[s], qbuf.at[t], q_send.at[t], q_recv.at[t], place(e, 0)))
            unit(s, 0)
            unit(s, 1)
            near.append(s)
    for e in range(1, Y):
        s = slot(-e, 0)
        got_q[s].wait_recv()
        unit(s, 0)
        unit(s, 1)
        near.append(s)
    for s in near:
        unit(s, 2)
    for c in got_r:
        c.wait_recv()
    for s in near:
        unit(s, 3)
    for i in range(C - 1):
        for e in range(1, Y):
            s = slot(-e, -(i + 1))
            got_q[s].wait_recv()
            for b in range(QUAD):
                unit(s, b)

    x = best[...]
    hi = x.astype(jnp.bfloat16)
    x = x - hi.astype(jnp.float32)
    mid = x.astype(jnp.bfloat16)
    low = (x - mid.astype(jnp.float32)).astype(jnp.bfloat16)
    sums = jnp.dot(low, ones[...], preferred_element_type=jnp.float32)
    sums += jnp.dot(mid, ones[...], preferred_element_type=jnp.float32)
    sums += jnp.dot(hi, ones[...], preferred_element_type=jnp.float32)
    sums = sums.reshape(G, per, sums.shape[1])
    sc_out[...] = sums
    sc_in[0] = sums[0]
    got_s = []
    for dy in range(Y):
        for dz in range(C):
            if dy or dz:
                s, t = slot(dy, dz), slot(-dy, -dz)
                got_s.append(go(copy(
                    sc_out.at[s], sc_in.at[t], s_send.at[t], s_recv.at[t], place(dy, dz)
                )))
    for c in got_s:
        c.wait_recv()

    def total(op, tiles):
        t = tiles[0]
        for g in range(1, G):
            t = op(t, tiles[g])
        shift = 1
        while shift < per:
            t = op(t, pltpu.roll(t, shift, 0))
            shift *= 2
        shift = per
        while shift < QUAD * per:
            t = op(t, pltpu.roll(t, shift, 1))
            shift *= 2
        return t

    tile = sc_in.shape[1:]
    lane = lax.broadcasted_iota(jnp.int32, tile, 1)
    doc = lax.broadcasted_iota(jnp.int32, tile, 0)
    kind = (lane // per) % QUAD
    owner = ((kind // 2 + side) % 2) * 2 + (kind % 2 + core) % 2
    want = jnp.zeros(tile, jnp.int32)
    for i in range(per):
        want = jnp.where(lane % per == i, pos_ref[i], want)
    scores, chosen = [], []
    for g in range(G):
        peer_y, peer_z = (y + g // C) % Y, (z + g % C) % C
        ids = ((peer_y * QUAD + owner) * C + peer_z) * per + doc
        tile_scores = sc_in[g]
        scores.append(tile_scores)
        chosen.append(jnp.where(ids == want, tile_scores, 0.0))
    peak = total(jnp.maximum, scores)
    expsum = total(jnp.add, [jnp.exp(t - peak) for t in scores])
    loss = peak + jnp.log(expsum) - total(jnp.add, chosen)
    out_ref[...] = loss[0:1, 0:per]
    for c in started:
        c.wait_send()


def local(Y, C, queries, documents, lengths, positives):
    per, QT, dim = queries.shape
    DT = documents.shape[1]
    G = Y * C
    dma = pltpu.SemaphoreType.DMA
    vmem = pl.BlockSpec(memory_space=pltpu.VMEM)
    smem = pl.BlockSpec(memory_space=pltpu.SMEM)
    out = pl.pallas_call(
        functools.partial(kernel, Y, C, per, QT, DT),
        out_shape=jax.ShapeDtypeStruct((1, per), jnp.float32),
        in_specs=[smem, smem, vmem, vmem],
        out_specs=vmem,
        scratch_shapes=[
            pltpu.VMEM((QUAD, per * DT, dim), jnp.bfloat16),
            pltpu.VMEM((G, per * QT, dim), jnp.bfloat16),
            pltpu.VMEM((G * per, QUAD * per * QT), jnp.float32),
            pltpu.VMEM((QUAD * per * QT, 128), jnp.bfloat16),
            pltpu.VMEM((G, per, 128), jnp.float32),
            pltpu.VMEM((G, per, 128), jnp.float32),
            dma, dma, dma((PARTS,)), dma((PARTS,)), dma((PARTS,)), dma((PARTS,)),
            dma((G,)), dma((G,)), dma((G,)), dma((G,)),
        ],
        compiler_params=pltpu.CompilerParams(collective_id=0, has_side_effects=True),
    )(
        lengths, positives,
        queries.reshape(per * QT, dim), documents.reshape(per * DT, dim),
    )
    return out.reshape(per)


def solution(mesh):
    Y, C = mesh.shape["row"] // QUAD, mesh.shape["col"]
    placed = (
        P(("row", "col"), None, None),
        P(("row", "col"), None, None),
        P(("row", "col")),
        P(("row", "col")),
    )
    return jax.shard_map(
        functools.partial(local, Y, C),
        mesh=mesh, in_specs=placed, out_specs=P(("row", "col")), check_vma=False,
    )
```

time: 68.8 us -> 25.9 us (0.38)
  Pallas kernels: 0 us -> 24.6 us
  blocking collectives: 23.8 us -> 0 us
  between operations: 14.1 us -> 0.02 us
  waiting for transfers between devices: 11.2 us -> 0 us
  matrix products: 8.9 us -> 0 us
  starting transfers between devices: 3.65 us -> 0 us
  other arithmetic: 3.1 us -> 0 us
  local copies, waits for them, and re-layouts: 3.55 us -> 1.1 us
    pallas_call x0 -> x1, Pallas kernels: none -> 24.6 us  [local(): pl.pallas_call(functools.partial(kernel, Y, C, per, QT, DT), out_shape=ja...]
    unnamed x1 -> x0, blocking collectives: 13.7 us -> none
    all_gather x1 -> x0, blocking collectives: 10.1 us -> none  [local(): lax.all_gather(queries, 'row', axis=0, tiled=True)]
    dot_general x4 -> x0, matrix products: 8.9 us -> none  [one_group(): lax.dot_general(query_flat, block_docs, (((1,), (1,)), ((), ())), preferr...]
    all_gather x1 -> x0, waiting for transfers between devices: 5.76 us -> none  [local(): lax.all_gather(documents, 'col', axis=0, tiled=True)]
    all_to_all x1 -> x0, waiting for transfers between devices: 4.7 us -> none  [local(): lax.all_to_all(block_scores, 'row', split_axis=0, concat_axis=1, tiled=True)]
    all_to_all x1 -> x0, starting transfers between devices: 3.64 us -> none  [local(): lax.all_to_all(block_scores, 'row', split_axis=0, concat_axis=1, tiled=True)]
    unnamed x7 -> x3, local copies, waits for them, and re-layouts: 2.25 us -> 1.1 us
  transfers between devices with their start and end apart: 2 -> 0, of which waited for: 2 -> 0; matrix products, arithmetic and copies ran while one was open for 3% -> 0% of each run, Pallas kernels for 0% -> 0%
where the time goes in v1:
time: 25.9 us; the launch traced here: 25.7 us
  Pallas kernels  24.6 us (95%)
  local copies, waits for them, and re-layouts  1.1 us (4%)
    pallas_call x1, Pallas kernels, local(): pl.pallas_call(functools.partial(kernel, Y, C, per, QT, DT), out_shape=ja...  24.6 us
    unnamed x3, local copies, waits for them, and re-layouts  1.1 us

profile of v1, /device:TPU:0, one launch (start us, length us, event | category | flops | bytes accessed | tf_op | source)
XLA Modules:
  0.0 25.7 jit_solution(4909789868276858476)
XLA Ops:
  0.0 24.6 %shard_map.46 = f32[1,8]{1,0:T(1,128)} custom-call(s32[8]{0:T(128)} %len_ref.1, s32[8]{0:T(128)} %pos_ref.1, bf16[256,128]{1,0:T(8,128)(2,1)} %bitcast.4, bf16[1024,128]{1,0:T(8,128)(2,1)} %bitcast.3), custom_call_target="tpu_custom_call" | custom-call | tf_op jit(solution)/shard_map/pallas_call | solution.py:194
  24.6 0.0 copy-start
  24.6 0.6 %copy-done = f32[1,8]{1,0:T(1,128)S(1)} copy-done((f32[1,8]{1,0:T(1,128)S(1)}, f32[1,8]{1,0:T(1,128)}, u32[]{:S(2)}) %copy-start) | copy-done | bytes 56
  25.2 0.5 %copy.6 = f32[8]{0:T(128)} copy(f32[8]{0:T(128)S(1)} %bitcast.5) | data formatting | bytes 64
Async XLA Ops:
  24.6 0.6 %copy-start = (f32[1,8]{1,0:T(1,128)S(1)}, f32[1,8]{1,0:T(1,128)}, u32[]{:S(2)}) copy-start(f32[1,8]{1,0:T(1,128)} %shard_map.46) | copy-start | bytes 100

commit v2 on v1

v2 whole, which is shorter than its diff:
```python
import functools

import jax
import jax.numpy as jnp
from jax import lax
from jax.experimental import pallas as pl
from jax.experimental.pallas import tpu as pltpu
from jax.sharding import PartitionSpec as P

MESH = pl.DeviceIdType.MESH
QUAD = 4
PARTS = 4
HALVES = 2


def kernel(
    Y, C, per, QT, DT,
    len_hbm, pos_hbm, q_hbm, d_hbm, out_ref,
    len_ref, pos_ref, d_ref, dbuf, qbuf, best, ones, sc_out, sc_in, in_sem,
    d_send, d_recv, x_send, x_recv, r_send, r_recv, q_send, q_recv, s_send, s_recv,
):
    row, z = lax.axis_index("row"), lax.axis_index("col")
    y, k = row // QUAD, row % QUAD
    core, side = k % 2, k // 2
    core_peer = (row + 1 - 2 * core, z)
    chip_peer = (row + 2 - 4 * side, z)
    G = Y * C
    rows = per * DT
    toks = per * QT
    part = rows // PARTS
    half = toks // HALVES

    def flip(place, d):
        bit, moved = 1, place
        while bit <= d:
            if d & bit:
                moved = moved + bit - 2 * bit * ((place // bit) % 2)
            bit *= 2
        return moved

    def at(dy, dz):
        return (flip(y, dy) * QUAD + k, flip(z, dz))

    def slot(dy, dz):
        return dy * C + dz

    barrier = pltpu.get_barrier_semaphore()
    peers = [core_peer, chip_peer]
    peers += [at(0, d) for d in range(1, C)] + [at(e, 0) for e in range(1, Y)]
    for peer in peers:
        pl.semaphore_signal(barrier, inc=1, device_id=peer, device_id_type=MESH)

    into = [
        pltpu.make_async_copy(len_hbm, len_ref, in_sem.at[0]),
        pltpu.make_async_copy(d_hbm, d_ref, in_sem.at[1]),
        pltpu.make_async_copy(q_hbm, qbuf.at[0], in_sem.at[2]),
        pltpu.make_async_copy(pos_hbm, pos_ref, in_sem.at[3]),
    ]
    for c in into:
        c.start()

    lane = lax.broadcasted_iota(jnp.int32, ones.shape, 1)
    tok = lax.broadcasted_iota(jnp.int32, ones.shape, 0)
    ones[...] = jnp.where(lane % (QUAD * per) == tok // QT, 1.0, 0.0).astype(jnp.bfloat16)

    for c in into:
        c.wait()
    slots = lax.broadcasted_iota(jnp.int32, (DT, d_ref.shape[1]), 0)
    for i in range(per):
        block = d_ref[i * DT:(i + 1) * DT, :].astype(jnp.float32)
        block = jnp.where(slots < len_ref[i], block, block[0:1, :])
        dbuf[0, i * DT:(i + 1) * DT, :] = block.astype(jnp.bfloat16)

    pl.semaphore_wait(barrier, len(peers))

    started = []

    def go(src, dst, send, recv, peer):
        c = pltpu.make_async_remote_copy(
            src_ref=src, dst_ref=dst, send_sem=send, recv_sem=recv,
            device_id=peer, device_id_type=MESH,
        )
        c.start()
        started.append(c)
        return c

    def piece(b, i):
        return dbuf.at[b, pl.ds(i * part, part), :]

    def tokens(s, h):
        return qbuf.at[s, pl.ds(h * half, half), :]

    far = list(range(C - 1, 0, -1))
    got_q = {}

    def send_q(src, s, h, peer):
        got_q[s, h] = go(
            tokens(src, h), tokens(s, h), q_send.at[s, h], q_recv.at[s, h], peer
        )

    for d in far:
        for h in range(HALVES):
            send_q(0, slot(0, d), h, at(0, d))
    for e in range(1, Y):
        for h in range(HALVES):
            send_q(0, slot(e, 0), h, at(e, 0))
    got_x = [
        go(piece(0, i), piece(2, i), x_send.at[i], x_recv.at[i], chip_peer)
        for i in range(PARTS)
    ]
    got_d = go(dbuf.at[0], dbuf.at[1], d_send, d_recv, core_peer)
    got_r = []

    def unit(s, b):
        sim = lax.dot_general(
            dbuf[b], qbuf[s], (((1,), (1,)), ((), ())), preferred_element_type=jnp.float32
        )
        top = jnp.max(sim.reshape(per, DT, toks), axis=1)
        best[s * per:(s + 1) * per, b * toks:(b + 1) * toks] = top

    got_s = []

    def send_scores(s, count):
        x = best[s * per:(s + count) * per, :]
        hi = x.astype(jnp.bfloat16)
        x = x - hi.astype(jnp.float32)
        mid = x.astype(jnp.bfloat16)
        low = (x - mid.astype(jnp.float32)).astype(jnp.bfloat16)
        sums = jnp.dot(low, ones[...], preferred_element_type=jnp.float32)
        sums += jnp.dot(mid, ones[...], preferred_element_type=jnp.float32)
        sums += jnp.dot(hi, ones[...], preferred_element_type=jnp.float32)
        sums = sums.reshape(count, per, sums.shape[1])
        for i in range(count):
            if s + i == 0:
                sc_in[0] = sums[0]
            else:
                sc_out[s + i] = sums[i]
        for i in range(count - 1, -1, -1):
            t = s + i
            if t:
                got_s.append(go(
                    sc_out.at[t], sc_in.at[t], s_send.at[t], s_recv.at[t], at(t // C, t % C)
                ))

    unit(0, 0)
    got_d.wait_recv()
    unit(0, 1)
    for i in range(max(PARTS, C - 1)):
        if i < C - 1:
            s = slot(0, far[i])
            for h in range(HALVES):
                got_q[s, h].wait_recv()
                for e in range(1, Y):
                    send_q(s, slot(e, far[i]), h, at(e, 0))
        if i < PARTS:
            got_x[i].wait_recv()
            got_r.append(
                go(piece(2, i), piece(3, i), r_send.at[i], r_recv.at[i], core_peer)
            )
        if i < C - 1:
            unit(s, 0)
            unit(s, 1)
    for e in range(1, Y):
        s = slot(e, 0)
        for h in range(HALVES):
            got_q[s, h].wait_recv()
        unit(s, 0)
        unit(s, 1)
    near = [slot(0, d) for d in range(C)] + [slot(e, 0) for e in range(1, Y)]
    for s in near:
        unit(s, 2)
    for c in got_r:
        c.wait_recv()
    for s in near:
        unit(s, 3)
    send_scores(0, C)
    for e in range(1, Y):
        send_scores(slot(e, 0), 1)
    for d in far:
        for e in range(1, Y):
            s = slot(e, d)
            for h in range(HALVES):
                got_q[s, h].wait_recv()
            for b in range(QUAD):
                unit(s, b)
            send_scores(s, 1)

    def total(op, tiles):
        t = tiles[0]
        for g in range(1, G):
            t = op(t, tiles[g])
        shift = 1
        while shift < per:
            t = op(t, pltpu.roll(t, shift, 0))
            shift *= 2
        shift = per
        while shift < QUAD * per:
            t = op(t, pltpu.roll(t, shift, 1))
            shift *= 2
        return t

    tile = sc_in.shape[1:]
    lane = lax.broadcasted_iota(jnp.int32, tile, 1)
    doc = lax.broadcasted_iota(jnp.int32, tile, 0)
    kind = (lane // per) % QUAD
    owner = ((kind // 2 + side) % 2) * 2 + (kind % 2 + core) % 2
    want = jnp.zeros(tile, jnp.int32)
    for i in range(per):
        want = jnp.where(lane % per == i, pos_ref[i], want)
    for c in got_s:
        c.wait_recv()
    scores, chosen = [], []
    for g in range(G):
        ids = ((flip(y, g // C) * QUAD + owner) * C + flip(z, g % C)) * per + doc
        tile_scores = sc_in[g]
        scores.append(tile_scores)
        chosen.append(jnp.where(ids == want, tile_scores, 0.0))
    peak = total(jnp.maximum, scores)
    expsum = total(jnp.add, [jnp.exp(t - peak) for t in scores])
    loss = peak + jnp.log(expsum) - total(jnp.add, chosen)
    out_ref[...] = loss[0:1, 0:per].reshape(per)
    for c in started:
        c.wait_send()


def local(Y, C, queries, documents, lengths, positives):
    per, QT, dim = queries.shape
    DT = documents.shape[1]
    G = Y * C
    dma = pltpu.SemaphoreType.DMA
    anywhere = pl.BlockSpec(memory_space=pl.ANY)
    return pl.pallas_call(
        functools.partial(kernel, Y, C, per, QT, DT),
        out_shape=jax.ShapeDtypeStruct((per,), jnp.float32),
        in_specs=[anywhere] * 4,
        out_specs=pl.BlockSpec(memory_space=pltpu.VMEM),
        scratch_shapes=[
            pltpu.SMEM((per,), jnp.int32),
            pltpu.SMEM((per,), jnp.int32),
            pltpu.VMEM((per * DT, dim), jnp.bfloat16),
            pltpu.VMEM((QUAD, per * DT, dim), jnp.bfloat16),
            pltpu.VMEM((G, per * QT, dim), jnp.bfloat16),
            pltpu.VMEM((G * per, QUAD * per * QT), jnp.float32),
            pltpu.VMEM((QUAD * per * QT, 128), jnp.bfloat16),
            pltpu.VMEM((G, per, 128), jnp.float32),
            pltpu.VMEM((G, per, 128), jnp.float32),
            dma((4,)),
            dma, dma, dma((PARTS,)), dma((PARTS,)), dma((PARTS,)), dma((PARTS,)),
            dma((G, HALVES)), dma((G, HALVES)), dma((G,)), dma((G,)),
        ],
        compiler_params=pltpu.CompilerParams(collective_id=0, has_side_effects=True),
    )(
        lengths, positives,
        queries.reshape(per * QT, dim), documents.reshape(per * DT, dim),
    )


def solution(mesh):
    Y, C = mesh.shape["row"] // QUAD, mesh.shape["col"]
    placed = (
        P(("row", "col"), None, None),
        P(("row", "col"), None, None),
        P(("row", "col")),
        P(("row", "col")),
    )
    return jax.shard_map(
        functools.partial(local, Y, C),
        mesh=mesh, in_specs=placed, out_specs=P(("row", "col")), check_vma=False,
    )
```

time: 25.9 us -> 24 us (0.927)
  Pallas kernels: 24.6 us -> 22.6 us
    pallas_call x1, Pallas kernels: 24.6 us -> 22.6 us  [local(): pl.pallas_call(functools.partial(kernel, Y, C, per, QT, DT), out_shape=ja...]
    unnamed x3 -> x1, local copies, waits for them, and re-layouts: 1.1 us -> 1.19 us
where the time goes in v2:
time: 24 us; the launch traced here: 23.8 us
  Pallas kernels  22.6 us (94%)
  local copies, waits for them, and re-layouts  1.19 us (5%)
    pallas_call x1, Pallas kernels, local(): pl.pallas_call(functools.partial(kernel, Y, C, per, QT, DT), out_shape=ja...  22.6 us
    unnamed x1, local copies, waits for them, and re-layouts  1.19 us

profile of v2, /device:TPU:0, one launch (start us, length us, event | category | flops | bytes accessed | tf_op | source)
XLA Modules:
  0.0 23.8 jit_solution(3621222878566399174)
XLA Ops:
  0.0 22.6 %shard_map.46 = f32[8]{0:T(128)} custom-call(s32[8]{0:T(128)} %len_hbm.1, s32[8]{0:T(128)} %pos_hbm.1, bf16[256,128]{1,0:T(8,128)(2,1)} %bitcast.3, bf16[1024,128]{1,0:T(8,128)(2,1)} %bitcast.2), custom_call_target="tpu_custom_call" | custom-call | tf_op jit(solution)/shard_map/pallas_call | solution.py:232
  22.6 1.2 %copy.6 = f32[8]{0:T(128)} copy(f32[8]{0:T(128)} %shard_map.46) | data formatting | bytes 64

commit v3 on v2

--- a/solution.py
+++ b/solution.py
@@ -145,6 +145,12 @@
     unit(0, 0)
     got_d.wait_recv()
     unit(0, 1)
+    for e in range(1, Y):
+        s = slot(e, 0)
+        for h in range(HALVES):
+            got_q[s, h].wait_recv()
+        unit(s, 0)
+        unit(s, 1)
     for i in range(max(PARTS, C - 1)):
         if i < C - 1:
             s = slot(0, far[i])
@@ -160,12 +166,6 @@
         if i < C - 1:
             unit(s, 0)
             unit(s, 1)
-    for e in range(1, Y):
-        s = slot(e, 0)
-        for h in range(HALVES):
-            got_q[s, h].wait_recv()
-        unit(s, 0)
-        unit(s, 1)
     near = [slot(0, d) for d in range(C)] + [slot(e, 0) for e in range(1, Y)]
     for s in near:
         unit(s, 2)

time: 24 us -> 23.7 us (0.987)
  Pallas kernels: 22.6 us -> 22.3 us
    pallas_call x1, Pallas kernels: 22.6 us -> 22.3 us  [local(): pl.pallas_call(functools.partial(kernel, Y, C, per, QT, DT), out_shape=ja...]
where the time goes in v3:
time: 23.7 us; the launch traced here: 23.5 us
  Pallas kernels  22.3 us (94%)
  local copies, waits for them, and re-layouts  1.19 us (5%)
    pallas_call x1, Pallas kernels, local(): pl.pallas_call(functools.partial(kernel, Y, C, per, QT, DT), out_shape=ja...  22.3 us
    unnamed x1, local copies, waits for them, and re-layouts  1.19 us

profile of v3, /device:TPU:0, one launch (start us, length us, event | category | flops | bytes accessed | tf_op | source)
XLA Modules:
  0.0 23.5 jit_solution(3022236407169835767)
XLA Ops:
  0.0 22.3 %shard_map.46 = f32[8]{0:T(128)} custom-call(s32[8]{0:T(128)} %len_hbm.1, s32[8]{0:T(128)} %pos_hbm.1, bf16[256,128]{1,0:T(8,128)(2,1)} %bitcast.3, bf16[1024,128]{1,0:T(8,128)(2,1)} %bitcast.2), custom_call_target="tpu_custom_call" | custom-call | tf_op jit(solution)/shard_map/pallas_call | solution.py:232
  22.3 1.2 %copy.6 = f32[8]{0:T(128)} copy(f32[8]{0:T(128)} %shard_map.46) | data formatting | bytes 64
